TPU v7x, 32 devices: a whole 2x2x4 slice. The times are simulated.
32 devices in a mesh: section: 4 (over y, core), img: 8 (over z, x).
Axes of the slice: x: 2, y: 2, z: 4, core: 2. Of those that a mesh axis runs over, the one named last changes fastest.
Arguments:
- early_feats: bfloat16 [8, 4096, 1280], P('section', 'img'), may hold values from -6 to 6
- final_embed: bfloat16 [8, 4096, 256], P('section', 'img'), may hold values from -240 to 240
- prompt_counts: int32 [8], replicated, may hold values from 16 to 64, as said below
- box_pixels: int32 [8, 64, 4], replicated, may hold values from 0 to 1023
- pair_table: int32 [8], replicated, may hold values from 0 to 7, as said below
- token_table: float32 [8, 256], replicated, may hold values from -6 to 6
- pe_basis: float32 [2, 128], replicated, may hold values from -5 to 5
- w_early: bfloat16 [1280, 256], replicated, may hold values from -0.15625 to 0.15625
- attend_in: bfloat16 [2, 6, 256, 128], replicated, may hold values from -0.375 to 0.375
- attend_out: bfloat16 [2, 2, 128, 256], replicated, may hold values from -0.5 to 0.5
- mlp_up: bfloat16 [2, 256, 2048], replicated, may hold values from -0.375 to 0.375
- mlp_down: bfloat16 [2, 2048, 256], replicated, may hold values from -0.125 to 0.125
- w_hyper: bfloat16 [256, 256], replicated, may hold values from -0.375 to 0.375
Outputs:
- masks: float32 [8, 64, 4096], P('section', None, 'img')
Inputs may be any that keep to these rules, and one draw needn't show every extreme that they name: `prompt_counts`: at least one image has all 64 prompts live. `pair_table`: a permutation of the images that maps all 2 images of an output group to the 2 images of one input group, in any order.
All inputs are finite; a program needn't handle non-finite values.
Results may differ from a plain program's by a relative error of at most 0.017.
The roundings to bfloat16 on the way count: a program that leaves them out, or rounds other values in their place, can miss the bound.
Values may be sent and summed in bfloat16 or wider, within the bound.
A program may use at most 64 MiB of HBM per device.

v0:
```python
import math

import jax
import jax.numpy as jnp
from jax import lax
from jax.sharding import PartitionSpec as P

HEADS = 8
GRID = 64
IMG_PIX = 1024
TOKS_P = 8
LAYERS = 2


NORM_EPS = 0.01


def partner(x, axis, distance):
    return lax.ppermute(x, axis, [(i, i ^ 1 << distance) for i in range(lax.axis_size(axis))])


def shortened(x):
    return jax.tree.map(lambda a: a.astype(jnp.bfloat16) if a.dtype == jnp.float32 else a, x)


def norm_rows(values):
    center = values - jnp.mean(values, axis=-1, keepdims=True)
    spread = jnp.mean(center * center, axis=-1, keepdims=True)
    return center / jnp.sqrt(spread + NORM_EPS)


def fourier(coord_x, coord_y, pe_basis):
    phase = (2.0 * coord_x - 1.0)[..., None] * pe_basis[0] + (2.0 * coord_y - 1.0)[
        ..., None
    ] * pe_basis[1]
    phase = 2.0 * math.pi * phase
    return jnp.concatenate([jnp.sin(phase), jnp.cos(phase)], axis=-1)


def grid_code(index, pe_basis):
    column = (index % GRID).astype(jnp.float32)
    row_idx = (index // GRID).astype(jnp.float32)
    return fourier((column + 0.5) / GRID, (row_idx + 0.5) / GRID, pe_basis)


def start_tokens(box_rows, token_table, pe_basis):
    coords = (box_rows.astype(jnp.float32) + 0.5) / IMG_PIX
    corner_one = fourier(coords[:, 0], coords[:, 1], pe_basis)
    corner_two = fourier(coords[:, 2], coords[:, 3], pe_basis)
    slots = jnp.arange(TOKS_P)[None, :, None]
    tokens = token_table[None] + jnp.where(slots == TOKS_P - 2, corner_one[:, None, :], 0.0)
    tokens = tokens + jnp.where(slots == TOKS_P - 1, corner_two[:, None, :], 0.0)
    return tokens.reshape(-1, token_table.shape[-1])


def bdot(left, right):
    return jnp.dot(left, right, preferred_element_type=jnp.float32)


def make_hq(early_part, w_early):
    hq_part = jax.nn.gelu(bdot(early_part, w_early), approximate=False).astype(jnp.bfloat16)
    return lax.optimization_barrier(hq_part)


def shards(
    early_feats,
    final_embed,
    prompt_counts,
    box_pixels,
    pair_table,
    token_table,
    pe_basis,
    w_early,
    attend_in,
    attend_out,
    mlp_up,
    mlp_down,
    w_hyper,
):
    images = early_feats.shape[0]
    pos_dev = early_feats.shape[1]
    width = final_embed.shape[2]
    prompts = box_pixels.shape[1]
    devices = lax.axis_size("img")
    my_index = lax.axis_index("img")
    my_section = lax.axis_index("section")
    img_bits = images.bit_length() - 1
    all_bits = devices.bit_length() - 1
    my_bit = my_index & 1

    def split_images(part):
        pairs = part.reshape(part.shape[0] // 2, 2, part.shape[1], width)
        keep = lax.dynamic_index_in_dim(pairs, my_bit, 1, keepdims=False)
        send = lax.dynamic_index_in_dim(pairs, 1 - my_bit, 1, keepdims=False)
        got = partner(send, "img", 0)
        lower = jnp.where(my_bit == 0, keep, got)
        upper = jnp.where(my_bit == 0, got, keep)
        return jnp.concatenate([lower, upper], axis=1)

    final_here = split_images(final_embed)
    hq_here = split_images(make_hq(early_feats, w_early))
    held = 1
    held_pos = images * pos_dev
    members = devices // images
    my_rank = my_index // images
    table_offset = my_index % images
    first_pos = my_rank * held_pos
    mine = my_section * images + table_offset
    my_counts = lax.dynamic_slice_in_dim(prompt_counts, mine, held, 0)
    my_boxes = lax.dynamic_slice_in_dim(box_pixels, mine, held, 0)
    per_image = prompts * TOKS_P
    rows_all = held * per_image
    own_rows = rows_all // members
    head_size = attend_in.shape[-1] // HEADS
    scale = head_size ** (-0.5)
    tokens_start = start_tokens(my_boxes.reshape(-1, 4), token_table, pe_basis)
    tok_own = lax.dynamic_slice_in_dim(tokens_start, my_rank * own_rows, own_rows, 0)
    positions = first_pos + jnp.arange(held_pos, dtype=jnp.int32)
    img_code = grid_code(positions, pe_basis)
    image = final_here.astype(jnp.float32)
    live_prompt = jnp.arange(prompts, dtype=jnp.int32)[None, :] < my_counts[:, None]
    live_token = jnp.repeat(live_prompt, TOKS_P, axis=1)
    query_one = bdot(tokens_start.astype(jnp.bfloat16), attend_in[0, 0]).astype(jnp.bfloat16)
    hyper = None
    for layer in range(LAYERS):
        image_bf = image.astype(jnp.bfloat16)
        key_bf = (image + img_code[None]).astype(jnp.bfloat16)
        keys_one = bdot(key_bf, attend_in[layer, 1]).astype(jnp.bfloat16)
        values_one = bdot(image_bf, attend_in[layer, 2]).astype(jnp.bfloat16)
        query_heads = query_one.reshape(held, per_image, HEADS, head_size)
        key_heads = keys_one.reshape(held, held_pos, HEADS, head_size)
        value_heads = values_one.reshape(held, held_pos, HEADS, head_size)
        scores = (
            jnp.einsum(
                "iqhd,ikhd->ihqk", query_heads, key_heads, preferred_element_type=jnp.float32
            )
            * scale
        )
        values = jnp.max(scores, axis=-1)
        for peak_bit in range(img_bits, all_bits):
            values = jnp.maximum(values, partner(values, "img", peak_bit))
        weights = jnp.exp(scores - values[..., None]).astype(jnp.bfloat16)
        summed = jnp.einsum(
            "ihqk,ikhd->iqhd", weights, value_heads, preferred_element_type=jnp.float32
        ).reshape(rows_all, HEADS * head_size)
        totals = jnp.sum(weights.astype(jnp.float32), axis=-1)
        totals = jnp.transpose(totals, (0, 2, 1)).reshape(rows_all, HEADS)
        reduce_summed = summed
        reduce_totals = totals
        for reduce_bit in reversed(range(img_bits, all_bits)):
            reduce_my_bit = my_index >> reduce_bit & 1
            split_s = reduce_summed.reshape(2, reduce_summed.shape[0] // 2, reduce_summed.shape[1])
            split_t = reduce_totals.reshape(2, reduce_totals.shape[0] // 2, reduce_totals.shape[1])
            keep_s = lax.dynamic_index_in_dim(split_s, reduce_my_bit, 0, keepdims=False)
            keep_t = lax.dynamic_index_in_dim(split_t, reduce_my_bit, 0, keepdims=False)
            send_s = lax.dynamic_index_in_dim(split_s, 1 - reduce_my_bit, 0, keepdims=False)
            send_t = lax.dynamic_index_in_dim(split_t, 1 - reduce_my_bit, 0, keepdims=False)
            reduce_got = (
                partner(send_s.astype(jnp.bfloat16), "img", reduce_bit).astype(send_s.dtype),
                partner(send_t.astype(jnp.bfloat16), "img", reduce_bit).astype(send_t.dtype),
            )
            reduce_summed = keep_s + reduce_got[0]
            reduce_totals = keep_t + reduce_got[1]
        first_out = (
            reduce_summed.reshape(own_rows, HEADS, head_size) / reduce_totals[:, :, None]
        ).reshape(own_rows, HEADS * head_size)
        tok_two = norm_rows(tok_own + bdot(first_out.astype(jnp.bfloat16), attend_out[layer, 0]))
        hidden = jax.nn.relu(bdot(tok_two.astype(jnp.bfloat16), mlp_up[layer])).astype(jnp.bfloat16)
        tok_three = norm_rows(tok_two + bdot(hidden, mlp_down[layer]))
        three_own = tok_three.astype(jnp.bfloat16)
        last_layer = layer == LAYERS - 1
        rows = (three_own,)
        for collect_bit in range(img_bits, all_bits):
            collect_my_bit = my_index >> collect_bit & 1
            collect_got = jax.tree.map(
                lambda part, own: part.astype(own.dtype),
                partner(shortened(rows), "img", collect_bit),
                rows,
            )
            rows = tuple(
                (
                    jnp.concatenate(
                        [
                            jnp.where(collect_my_bit == 0, mine, theirs),
                            jnp.where(collect_my_bit == 0, theirs, mine),
                        ],
                        axis=0,
                    )
                    for mine, theirs in zip(rows, collect_got)
                )
            )
        three_all = rows[0]
        keys_two = bdot(three_all, attend_in[layer, 4]).astype(jnp.bfloat16)
        values_two = bdot(three_all, attend_in[layer, 5]).astype(jnp.bfloat16)
        if last_layer:
            hyper = bdot(three_all.reshape(-1, TOKS_P, width)[:, TOKS_P - 3], w_hyper).astype(
                jnp.bfloat16
            )
        else:
            query_one = bdot(three_all, attend_in[layer + 1, 0]).astype(jnp.bfloat16)
        query_two = (
            bdot(key_bf, attend_in[layer, 3])
            .astype(jnp.bfloat16)
            .reshape(held, held_pos, HEADS, head_size)
        )
        token_keys = keys_two.reshape(held, per_image, HEADS, head_size)
        token_values = values_two.reshape(held, per_image, HEADS, head_size)
        scores_two = (
            jnp.einsum("ikhd,iqhd->ihkq", query_two, token_keys, preferred_element_type=jnp.float32)
            * scale
        )
        scores_two = jnp.where(live_token[:, None, None, :], scores_two, -jnp.inf)
        highest_two = jnp.max(scores_two, axis=-1, keepdims=True)
        weights_two = jnp.exp(scores_two - highest_two).astype(jnp.bfloat16)
        summed_two = jnp.einsum(
            "ihkq,iqhd->ikhd", weights_two, token_values, preferred_element_type=jnp.float32
        )
        totals_two = jnp.transpose(jnp.sum(weights_two.astype(jnp.float32), axis=-1), (0, 2, 1))
        second_out = (summed_two / totals_two[..., None]).reshape(held, held_pos, HEADS * head_size)
        image = norm_rows(image + bdot(second_out.astype(jnp.bfloat16), attend_out[layer, 1]))
        tok_own = tok_three
    hyper_rows = hyper.reshape(held, prompts, width)
    mask_feats = (image + hq_here.astype(jnp.float32)).astype(jnp.bfloat16)
    logits = jnp.einsum(
        "ipc,ikc->ipk", hyper_rows, mask_feats, preferred_element_type=jnp.float32
    ) * width ** (-0.5)
    result = jnp.where(live_prompt[:, :, None], logits, 0.0).astype(jnp.bfloat16)
    for bit in reversed(range(img_bits)):
        my_bit = my_index >> bit & 1
        halves = result.reshape(result.shape[0], prompts, 2, result.shape[2] // 2)
        keep = lax.dynamic_index_in_dim(halves, my_bit, 2, keepdims=False)
        send = lax.dynamic_index_in_dim(halves, 1 - my_bit, 2, keepdims=False)
        got = partner(send, "img", bit)
        first = jnp.where(my_bit == 0, keep, got)
        second = jnp.where(my_bit == 0, got, keep)
        result = jnp.stack([first, second], axis=1).reshape(
            2 * keep.shape[0], prompts, keep.shape[2]
        )
    gathered = lax.all_gather(result, "section", axis=0, tiled=True)
    outputs = lax.dynamic_slice_in_dim(pair_table, my_section * images, images, 0)
    return jnp.concatenate(
        [
            lax.dynamic_slice_in_dim(gathered, outputs[i], 1, 0).astype(jnp.float32)
            for i in range(images)
        ]
    )


def solution(mesh):
    placed = (
        P("section", "img", None),
        P("section", "img", None),
        P(),
        P(),
        P(),
        P(),
        P(),
        P(),
        P(),
        P(),
        P(),
        P(),
        P(),
    )
    return jax.shard_map(
        shards, mesh=mesh, in_specs=placed, out_specs=P("section", None, "img"), check_vma=False
    )
```

profile of v0, /device:TPU:0, one launch (start us, length us, event | category | flops | bytes accessed | tf_op | source)
XLA Modules:
  0.0 173.7 jit_solution(10622891999079575566)
XLA Ops:
  0.0 1.2 constant_dynamic-slice_fusion.12
  1.4 3.0 %collective-permute-start = (bf16[1,512,256]{1,2,0:T(8,128)(2,1)S(1)}, bf16[1,512,256]{1,2,0:T(8,128)(2,1)}, u32[]{:S(2)}, u32[]{:S(2)}) collective-permute-start(bf16[1,512,256]{1,2,0:T(8,128)(2,1)S(1)} %copy.68), channel_id=1, source_target_pairs={{0,1},{1,0},{2,3},{3,2},{4,5},{5,4},{6,7},{7,6},{8,9},{9,8},{10,11... | collective-permute-start | bytes 786440 | tf_op jit(solution)/shard_map/ppermute | solution.py:19
  7.9 5.0 %fusion.21 = bf16[2,512,256]{1,2,0:T(8,128)(2,1)} fusion(bf16[2,512,1280]{2,1,0:T(8,128)(2,1)S(1)} %copy-done, bf16[1280,256]{1,0:T(8,128)(2,1)} %param.20), kind=kOutput, calls=%fused_computation.57 | convolution fusion | flops 688128000 | bytes 3801088 | tf_op jit(solution)/shard_map/dot_general | solution.py:57
  12.9 1.2 convolution_convert_fusion.11
  14.2 2.0 %fusion.48 = (f32[1024,128]{0,1:T(8,128)S(1)}, f32[1024,128]{0,1:T(8,128)S(1)}) fusion(f32[128]{0:T(128)S(1)} %get-tuple-element.42, f32[1024]{0:T(1024)S(1)} %get-tuple-element.66, f32[128]{0:T(128)S(1)} %get-tuple-element.41, f32[1024]{0:T(1024)S(1)} %get-tuple-element.65), kind=kLoop, calls=%fused_computation.97 | loop fusion | flops 524288 | bytes 1057792 | tf_op jit(solution)/shard_map/sin | solution.py:37
  17.4 1.1 convolution_convert_fusion.4
  18.5 8.1 %multiply_reduce_fusion.1 = (f32[8,512]{1,0:T(8,128)S(1)}, f32[8,512,1024]{2,1,0:T(8,128)}) fusion(bf16[512,8,16]{0,2,1:T(8,128)(2,1)S(1)} %bitcast.324, bf16[1024,8,16]{0,2,1:T(8,128)(2,1)S(1)} %bitcast.308), kind=kOutput, calls=%fused_computation.11 | convolution fusion | flops 142602240 | bytes 17186816 | tf_op jit(solution)/shard_map/iqhd,ikhd->ihqk/dot_general | solution.py:134
  26.6 1.6 collective-permute-start.1
  30.4 2.7 %collective-permute-start.2 = (f32[1,8,512]{2,1,0:T(8,128)S(1)}, f32[1,8,512]{2,1,0:T(8,128)S(1)}, u32[]{:S(2)}, u32[]{:S(2)}) collective-permute-start(f32[1,8,512]{2,1,0:T(8,128)S(1)} %bitcast_maximum_fusion.1), channel_id=1, source_target_pairs={{0,4},{1,5},{2,6},{3,7},{4,0},{5,1},{6,2},{7,3},{8,12},{9,13},{10,... | collective-permute-start | bytes 49160 | tf_op jit(solution)/shard_map/ppermute | solution.py:19
  33.0 1.9 %convolution_convert_fusion.5 = bf16[1024,128]{0,1:T(8,128)(2,1)S(1)} fusion(bf16[1,512,256]{1,2,0:T(8,128)(2,1)S(1)} %get-tuple-element.14, bf16[1,512,256]{1,2,0:T(8,128)(2,1)S(1)} %get-tuple-element.13, bf16[2,6,256,128]{3,2,1,0:T(8,128)(2,1)} %param.21), kind=kOutput, calls=%fused_computation.37 | convolution fusion | flops 68288512 | bytes 851968 | tf_op jit(solution)/shard_map/dot_general | solution.py:57
  35.1 7.7 %convert_reduce_fusion.3 = f32[8,512]{1,0:T(8,128)S(1)} fusion(f32[8,512]{1,0:T(8,128)S(1)} %maximum_bitcast_fusion.4, f32[8,512,1024]{2,1,0:T(8,128)} %get-tuple-element.46), kind=kLoop, calls=%fused_computation.8 | loop fusion | flops 20967424 | bytes 16809984 | tf_op jit(solution)/shard_map/reduce_sum | solution.py:146
  42.8 3.4 %fusion.14 = f32[1,512,8,16]{1,3,2,0:T(8,128)S(1)} fusion(bf16[1024,8,16]{0,2,1:T(8,128)(2,1)S(1)} %bitcast.317, f32[8,512,1024]{2,1,0:T(8,128)S(1)} %copy-done.2, f32[8,512]{1,0:T(8,128)S(1)} %maximum_bitcast_fusion.4), kind=kOutput, calls=%fused_computation.41 | convolution fusion | flops 146800640 | bytes 17317888 | tf_op jit(solution)/shard_map/ihqk,ikhd->iqhd/dot_general | solution.py:143
  46.6 2.7 %collective-permute-start.3 = (bf16[256,128]{1,0:T(8,128)(2,1)S(1)}, bf16[256,128]{1,0:T(8,128)(2,1)S(1)}, u32[]{:S(2)}, u32[]{:S(2)}) collective-permute-start(bf16[256,128]{1,0:T(8,128)(2,1)S(1)} %bitcast.329), channel_id=1, source_target_pairs={{0,4},{1,5},{2,6},{3,7},{4,0},{5,1},{6,2},{7,3},{8,12},{9,13},{10,... | collective-permute-start | bytes 196616 | tf_op jit(solution)/shard_map/ppermute | solution.py:19
  50.4 4.3 %collective-permute-done.5 = bf16[256,8]{0,1:T(8,128)(2,1)} collective-permute-done((bf16[256,8]{0,1:T(8,128)(2,1)}, bf16[256,8]{0,1:T(8,128)(2,1)}, u32[]{:S(2)}, u32[]{:S(2)}) %collective-permute-start.5) | collective-permute-done | bytes 4128 | tf_op jit(solution)/shard_map/ppermute | solution.py:19
  55.4 1.6 collective-permute-start.6
  57.5 1.5 collective-permute-done.6
  59.1 1.9 %collective-permute-done.4 = bf16[128,128]{1,0:T(8,128)(2,1)S(1)} collective-permute-done((bf16[128,128]{1,0:T(8,128)(2,1)S(1)}, bf16[128,128]{1,0:T(8,128)(2,1)S(1)}, u32[]{:S(2)}, u32[]{:S(2)}) %collective-permute-start.4) | collective-permute-done | bytes 32800 | tf_op jit(solution)/shard_map/ppermute | solution.py:19
  61.0 1.2 fusion.160
  62.5 2.2 %fusion.161 = (f32[128]{0:T(128)S(1)}, f32[128,256]{1,0:T(8,128)S(1)}) fusion(bf16[2,2048,256]{2,1,0:T(8,128)(2,1)} %param.24, bf16[2,256,2048]{2,1,0:T(8,128)(2,1)} %param.23, f32[128,256]{1,0:T(8,128)S(1)} %get-tuple-element.48, f32[128]{0:T(128)S(1)} %add_sqrt_fusion.5, f32[128]{0:T(128)S(1)} %broadcast_multiply_fusion.5), kind=kOutput, calls=%fused_computation.303 | convolution fusion | flops 269188992 | bytes 2492928 | tf_op jit(solution)/shard_map/dot_general | solution.py:57
  66.4 3.2 %collective-permute-done.7 = bf16[128,256]{1,0:T(8,128)(2,1)S(1)} collective-permute-done((bf16[128,256]{1,0:T(8,128)(2,1)S(1)}, bf16[128,256]{1,0:T(8,128)(2,1)S(1)}, u32[]{:S(2)}, u32[]{:S(2)}) %collective-permute-start.7) | collective-permute-done | bytes 65568 | tf_op jit(solution)/shard_map/ppermute | solution.py:19
  71.9 4.8 %collective-permute-done.8 = bf16[256,256]{1,0:T(8,128)(2,1)S(1)} collective-permute-done((bf16[256,256]{1,0:T(8,128)(2,1)S(1)}, bf16[256,256]{1,0:T(8,128)(2,1)S(1)}, u32[]{:S(2)}, u32[]{:S(2)}) %collective-permute-start.8) | collective-permute-done | bytes 131104 | tf_op jit(solution)/shard_map/ppermute | solution.py:19
  79.9 3.1 %fusion = (f32[8,1024]{1,0:T(8,128)S(1)}, f32[8,1024,512]{1,2,0:T(8,128)S(1)}) fusion(pred[512]{0:T(512)(128)(4,1)S(1)} %broadcast_in_dim.133, bf16[1024,8,16]{0,2,1:T(8,128)(2,1)S(1)} %bitcast.307, bf16[512,8,16]{0,2,1:T(8,128)(2,1)S(1)} %bitcast.326), kind=kOutput, calls=%fused_computation.12 | convolution fusion | flops 146792448 | bytes 17203712 | tf_op jit(solution)/shard_map/ikhd,iqhd->ihkq/dot_general | solution.py:209
  83.1 4.2 %convert_reduce_fusion.2 = (f32[8,1024]{1,0:T(8,128)S(1)}, bf16[8,1024,512]{1,2,0:T(8,128)(2,1)S(1)}) fusion(f32[8,1024]{1,0:T(8,128)S(1)} %get-tuple-element.51, f32[8,1024,512]{1,2,0:T(8,128)S(1)} %get-tuple-element.52, pred[512]{0:T(512)(128)(4,1)S(1)} %broadcast_in_dim.133), kind=kLoop, calls=%fused_computation.5 | loop fusion | flops 25157632 | bytes 25231872 | tf_op jit(solution)/shard_map/reduce_sum | solution.py:218
  87.3 1.2 fusion.10
  89.2 1.1 convolution_convert_fusion.1
  90.4 8.1 %multiply_reduce_fusion = (f32[8,512]{1,0:T(8,128)S(1)}, f32[8,512,1024]{2,1,0:T(8,128)}) fusion(bf16[512,8,16]{0,2,1:T(8,128)(2,1)S(1)} %bitcast.323, bf16[1024,8,16]{0,2,1:T(8,128)(2,1)S(1)} %bitcast.309), kind=kOutput, calls=%fused_computation.10 | convolution fusion | flops 142602240 | bytes 17186816 | tf_op jit(solution)/shard_map/iqhd,ikhd->ihqk/dot_general | solution.py:134
  99.1 1.4 dynamic_slice.103
  100.5 1.7 collective-permute-done.9
  102.2 1.9 %convolution_convert_fusion.2 = bf16[1024,128]{0,1:T(8,128)(2,1)S(1)} fusion(bf16[2,6,256,128]{3,2,1,0:T(8,128)(2,1)} %param.21, f32[1024,256]{0,1:T(8,128)S(1)} %get-tuple-element.54, f32[1024]{0:T(1024)S(1)} %add_sqrt_fusion.1, f32[1024]{0:T(1024)S(1)} %broadcast_multiply_fusion.1), kind=kOutput, calls=%fused_computation.34 | convolution fusion | flops 68026368 | bytes 1384448 | tf_op jit(solution)/shard_map/dot_general | solution.py:57
  104.1 2.8 %collective-permute-done.10 = f32[1,8,512]{2,1,0:T(8,128)S(1)} collective-permute-done((f32[1,8,512]{2,1,0:T(8,128)S(1)}, f32[1,8,512]{2,1,0:T(8,128)S(1)}, u32[]{:S(2)}, u32[]{:S(2)}) %collective-permute-start.10) | collective-permute-done | bytes 16416 | tf_op jit(solution)/shard_map/ppermute | solution.py:19
  106.9 7.9 %convert_reduce_fusion.1 = f32[8,512]{1,0:T(8,128)S(1)} fusion(f32[8,512]{1,0:T(8,128)S(1)} %maximum_bitcast_fusion.3, f32[8,512,1024]{2,1,0:T(8,128)} %get-tuple-element.56), kind=kLoop, calls=%fused_computation.3 | loop fusion | flops 20967424 | bytes 16809984 | tf_op jit(solution)/shard_map/reduce_sum | solution.py:146
  114.7 3.3 %fusion.13 = f32[1,512,8,16]{1,3,2,0:T(8,128)S(1)} fusion(bf16[1024,8,16]{0,2,1:T(8,128)(2,1)S(1)} %bitcast.318, f32[8,512,1024]{2,1,0:T(8,128)S(1)} %copy-done.3, f32[8,512]{1,0:T(8,128)S(1)} %maximum_bitcast_fusion.3), kind=kOutput, calls=%fused_computation.40 | convolution fusion | flops 146800640 | bytes 17317888 | tf_op jit(solution)/shard_map/ihqk,ikhd->iqhd/dot_general | solution.py:143
  118.7 3.0 %collective-permute-start.11 = (bf16[256,128]{1,0:T(8,128)(2,1)S(1)}, bf16[256,128]{1,0:T(8,128)(2,1)S(1)}, u32[]{:S(2)}, u32[]{:S(2)}) collective-permute-start(bf16[256,128]{1,0:T(8,128)(2,1)S(1)} %bitcast.331), channel_id=1, source_target_pairs={{0,4},{1,5},{2,6},{3,7},{4,0},{5,1},{6,2},{7,3},{8,12},{9,13},{10,... | collective-permute-start | bytes 196616 | tf_op jit(solution)/shard_map/ppermute | solution.py:19
  121.8 1.2 collective-permute-done.13
  123.4 1.1 collective-permute-done.11
  125.1 1.5 collective-permute-done.14
  126.7 1.9 %collective-permute-done.12 = bf16[128,128]{1,0:T(8,128)(2,1)S(1)} collective-permute-done((bf16[128,128]{1,0:T(8,128)(2,1)S(1)}, bf16[128,128]{1,0:T(8,128)(2,1)S(1)}, u32[]{:S(2)}, u32[]{:S(2)}) %collective-permute-start.12) | collective-permute-done | bytes 32800 | tf_op jit(solution)/shard_map/ppermute | solution.py:19
  129.8 2.2 %fusion.168 = (f32[128]{0:T(128)S(1)}, f32[128,256]{1,0:T(8,128)S(1)}) fusion(bf16[2,2048,256]{2,1,0:T(8,128)(2,1)} %param.24, bf16[2,256,2048]{2,1,0:T(8,128)(2,1)} %param.23, f32[128,256]{1,0:T(8,128)S(1)} %get-tuple-element.58, f32[128]{0:T(128)S(1)} %add_sqrt_fusion.3, f32[128]{0:T(128)S(1)} %broadcast_multiply_fusion.3), kind=kOutput, calls=%fused_computation.306 | convolution fusion | flops 269188992 | bytes 2492928 | tf_op jit(solution)/shard_map/dot_general | solution.py:57
  133.0 3.7 %collective-permute-done.15 = bf16[128,256]{1,0:T(8,128)(2,1)S(1)} collective-permute-done((bf16[128,256]{1,0:T(8,128)(2,1)S(1)}, bf16[128,256]{1,0:T(8,128)(2,1)S(1)}, u32[]{:S(2)}, u32[]{:S(2)}) %collective-permute-start.15) | collective-permute-done | bytes 65568 | tf_op jit(solution)/shard_map/ppermute | solution.py:19
  136.8 2.6 %collective-permute-start.16 = (bf16[256,256]{1,0:T(8,128)(2,1)S(1)}, bf16[256,256]{1,0:T(8,128)(2,1)S(1)}, u32[]{:S(2)}, u32[]{:S(2)}) collective-permute-start(bf16[256,256]{1,0:T(8,128)(2,1)S(1)} %pad_maximum_fusion.5), channel_id=1, source_target_pairs={{0,4},{1,5},{2,6},{3,7},{4,0},{5,1},{6,2},{7,3},{8,12},{9,13},{10,... | collective-permute-start | bytes 393224 | tf_op jit(solution)/shard_map/ppermute | solution.py:19
  140.5 3.6 %collective-permute-done.16 = bf16[256,256]{1,0:T(8,128)(2,1)S(1)} collective-permute-done((bf16[256,256]{1,0:T(8,128)(2,1)S(1)}, bf16[256,256]{1,0:T(8,128)(2,1)S(1)}, u32[]{:S(2)}, u32[]{:S(2)}) %collective-permute-start.16) | collective-permute-done | bytes 131104 | tf_op jit(solution)/shard_map/ppermute | solution.py:19
  146.4 3.1 %fusion.1 = (f32[8,1024]{1,0:T(8,128)S(1)}, f32[8,1024,512]{1,2,0:T(8,128)S(1)}) fusion(pred[512]{0:T(512)(128)(4,1)S(1)} %broadcast_in_dim.133, bf16[1024,8,16]{0,2,1:T(8,128)(2,1)S(1)} %bitcast.306, bf16[512,8,16]{0,2,1:T(8,128)(2,1)S(1)} %bitcast.325), kind=kOutput, calls=%fused_computation.13 | convolution fusion | flops 146792448 | bytes 17203712 | tf_op jit(solution)/shard_map/ikhd,iqhd->ihkq/dot_general | solution.py:209
  149.6 4.2 %convert_reduce_fusion = (f32[8,1024]{1,0:T(8,128)S(1)}, bf16[8,1024,512]{1,2,0:T(8,128)(2,1)S(1)}) fusion(f32[8,1024]{1,0:T(8,128)S(1)} %get-tuple-element.61, f32[8,1024,512]{1,2,0:T(8,128)S(1)} %get-tuple-element.62, pred[512]{0:T(512)(128)(4,1)S(1)} %broadcast_in_dim.133), kind=kLoop, calls=%fused_computation | loop fusion | flops 25157632 | bytes 25231872 | tf_op jit(solution)/shard_map/reduce_sum | solution.py:218
  153.8 1.2 fusion.11
  155.0 2.2 %fusion.173 = (f32[1024]{0:T(1024)S(1)}, f32[1024,256]{0,1:T(8,128)}) fusion(bf16[1024,128]{0,1:T(8,128)(2,1)S(1)} %bitcast.312, bf16[2,2,128,256]{3,2,1,0:T(8,128)(2,1)} %param.22, f32[1024]{0:T(1024)S(1)} %add_sqrt_fusion.1, f32[1024,256]{0,1:T(8,128)S(1)} %copy-done.5, f32[1024]{0:T(1024)S(1)} %broadcast_multiply_fusion.1), kind=kOutput, calls=%fused_computation.307 | convolution fusion | flops 68156416 | bytes 2437120 | tf_op jit(solution)/shard_map/dot_general | solution.py:57
  157.2 1.4 multiply_reduce_fusion.2
  158.5 1.6 fusion.15
  165.7 7.2 %all-gather = bf16[1,8,64,512]{3,2,0,1:T(8,128)(2,1)S(1)} all-gather(bf16[1,2,64,512]{3,2,0,1:T(8,128)(2,1)S(1)} %maximum_bitcast_fusion.2), channel_id=2, replica_groups=mesh['section'=4,'img'=8] {'section'}, dimensions={1}, use_global_device_ids=true | all-gather | bytes 655360 | tf_op jit(solution)/shard_map/all_gather | solution.py:239
  (151 shorter events, 29.0 us)
Async XLA Ops:
  0.0 7.9 %copy-start = (bf16[2,512,1280]{2,1,0:T(8,128)(2,1)S(1)}, bf16[2,512,1280]{2,1,0:T(8,128)(2,1)}, u32[]{:S(2)}) copy-start(bf16[2,512,1280]{2,1,0:T(8,128)(2,1)} %param.13) | copy-start | bytes 7864324
  0.0 12.9 %copy-start.9 = (f32[8,256]{1,0:T(8,128)S(1)}, f32[8,256]{1,0:T(8,128)}, u32[]{:S(2)}) copy-start(f32[8,256]{1,0:T(8,128)} %param.18) | copy-start | bytes 24580
  1.4 14.9 %collective-permute-start = (bf16[1,512,256]{1,2,0:T(8,128)(2,1)S(1)}, bf16[1,512,256]{1,2,0:T(8,128)(2,1)}, u32[]{:S(2)}, u32[]{:S(2)}) collective-permute-start(bf16[1,512,256]{1,2,0:T(8,128)(2,1)S(1)} %copy.68), channel_id=1, source_target_pairs={{0,1},{1,0},{2,3},{3,2},{4,5},{5,4},{6,7},{7,6},{8,9},{9,8},{10,11... | collective-permute-start | bytes 786440 | tf_op jit(solution)/shard_map/ppermute | solution.py:19
  12.9 16.8 %copy-start.15 = (s32[8]{0:T(128)S(1)}, s32[8]{0:T(128)}, u32[]{:S(2)}) copy-start(s32[8]{0:T(128)} %param.15) | copy-start | bytes 100
  26.6 3.8 %collective-permute-start.1 = (f32[1,8,512]{2,1,0:T(8,128)S(1)}, f32[1,8,512]{2,1,0:T(8,128)S(1)}, u32[]{:S(2)}, u32[]{:S(2)}) collective-permute-start(f32[1,8,512]{2,1,0:T(8,128)S(1)} %bitcast.327), channel_id=1, source_target_pairs={{0,2},{1,3},{2,0},{3,1},{4,6},{5,7},{6,4},{7,5},{8,10},{9,11},{10,... | collective-permute-start | bytes 49160 | tf_op jit(solution)/shard_map/ppermute | solution.py:19
  30.3 12.4 %copy-start.2 = (f32[8,512,1024]{2,1,0:T(8,128)S(1)}, f32[8,512,1024]{2,1,0:T(8,128)}, u32[]{:S(2)}) copy-start(f32[8,512,1024]{2,1,0:T(8,128)} %get-tuple-element.46) | copy-start | bytes 50331652
  30.4 4.7 %collective-permute-start.2 = (f32[1,8,512]{2,1,0:T(8,128)S(1)}, f32[1,8,512]{2,1,0:T(8,128)S(1)}, u32[]{:S(2)}, u32[]{:S(2)}) collective-permute-start(f32[1,8,512]{2,1,0:T(8,128)S(1)} %bitcast_maximum_fusion.1), channel_id=1, source_target_pairs={{0,4},{1,5},{2,6},{3,7},{4,0},{5,1},{6,2},{7,3},{8,12},{9,13},{10,... | collective-permute-start | bytes 49160 | tf_op jit(solution)/shard_map/ppermute | solution.py:19
  35.1 26.0 %copy-start.8 = (bf16[2,2,128,256]{3,2,1,0:T(8,128)(2,1)S(1)}, bf16[2,2,128,256]{3,2,1,0:T(8,128)(2,1)}, u32[]{:S(2)}) copy-start(bf16[2,2,128,256]{3,2,1,0:T(8,128)(2,1)} %param.22) | copy-start | bytes 786436
  46.6 10.4 %collective-permute-start.3 = (bf16[256,128]{1,0:T(8,128)(2,1)S(1)}, bf16[256,128]{1,0:T(8,128)(2,1)S(1)}, u32[]{:S(2)}, u32[]{:S(2)}) collective-permute-start(bf16[256,128]{1,0:T(8,128)(2,1)S(1)} %bitcast.329), channel_id=1, source_target_pairs={{0,4},{1,5},{2,6},{3,7},{4,0},{5,1},{6,2},{7,3},{8,12},{9,13},{10,... | collective-permute-start | bytes 196616 | tf_op jit(solution)/shard_map/ppermute | solution.py:19
  49.9 4.8 %collective-permute-start.5 = (bf16[256,8]{0,1:T(8,128)(2,1)}, bf16[256,8]{0,1:T(8,128)(2,1)}, u32[]{:S(2)}, u32[]{:S(2)}) collective-permute-start(bf16[256,8]{0,1:T(8,128)(2,1)} %fusion.133), channel_id=1, source_target_pairs={{0,4},{1,5},{2,6},{3,7},{4,0},{5,1},{6,2},{7,3},{8,12},{9,13},{10,... | collective-permute-start | bytes 12296 | tf_op jit(solution)/shard_map/ppermute | solution.py:19
  55.4 3.6 %collective-permute-start.6 = (bf16[128,8]{0,1:T(8,128)(2,1)S(1)}, bf16[128,8]{0,1:T(8,128)(2,1)S(1)}, u32[]{:S(2)}, u32[]{:S(2)}) collective-permute-start(bf16[128,8]{0,1:T(8,128)(2,1)S(1)} %fusion.141), channel_id=1, source_target_pairs={{0,2},{1,3},{2,0},{3,1},{4,6},{5,7},{6,4},{7,5},{8,10},{9,11},{10,... | collective-permute-start | bytes 6152 | tf_op jit(solution)/shard_map/ppermute | solution.py:19
  57.1 4.0 %collective-permute-start.4 = (bf16[128,128]{1,0:T(8,128)(2,1)S(1)}, bf16[128,128]{1,0:T(8,128)(2,1)S(1)}, u32[]{:S(2)}, u32[]{:S(2)}) collective-permute-start(bf16[128,128]{1,0:T(8,128)(2,1)S(1)} %fusion.107), channel_id=1, source_target_pairs={{0,2},{1,3},{2,0},{3,1},{4,6},{5,7},{6,4},{7,5},{8,10},{9,11},{10,... | collective-permute-start | bytes 98312 | tf_op jit(solution)/shard_map/ppermute | solution.py:19
  64.9 22.4 %copy-start.10 = (f32[128]{0:T(128)}, f32[128]{0:T(128)S(1)}, u32[]{:S(2)}) copy-start(f32[128]{0:T(128)S(1)} %add_sqrt_fusion.4) | copy-start | bytes 1540
  65.0 4.6 %collective-permute-start.7 = (bf16[128,256]{1,0:T(8,128)(2,1)S(1)}, bf16[128,256]{1,0:T(8,128)(2,1)S(1)}, u32[]{:S(2)}, u32[]{:S(2)}) collective-permute-start(bf16[128,256]{1,0:T(8,128)(2,1)S(1)} %fusion.158), channel_id=1, source_target_pairs={{0,2},{1,3},{2,0},{3,1},{4,6},{5,7},{6,4},{7,5},{8,10},{9,11},{10,... | collective-permute-start | bytes 196616 | tf_op jit(solution)/shard_map/ppermute | solution.py:19
  66.2 21.1 %copy-start.12 = (pred[64]{0:T(512)(128)(4,1)}, pred[64]{0:T(512)(128)(4,1)S(1)}, u32[]{:S(2)}) copy-start(pred[64]{0:T(512)(128)(4,1)S(1)} %iota_compare_fusion.2) | copy-start | bytes 196
  69.7 6.9 %collective-permute-start.8 = (bf16[256,256]{1,0:T(8,128)(2,1)S(1)}, bf16[256,256]{1,0:T(8,128)(2,1)S(1)}, u32[]{:S(2)}, u32[]{:S(2)}) collective-permute-start(bf16[256,256]{1,0:T(8,128)(2,1)S(1)} %pad_maximum_fusion.4), channel_id=1, source_target_pairs={{0,4},{1,5},{2,6},{3,7},{4,0},{5,1},{6,2},{7,3},{8,12},{9,13},{10,... | collective-permute-start | bytes 393224 | tf_op jit(solution)/shard_map/ppermute | solution.py:19
  87.3 11.2 %copy-start.6 = (bf16[2,512,256]{1,2,0:T(8,128)(2,1)S(1)}, bf16[2,512,256]{1,2,0:T(8,128)(2,1)}, u32[]{:S(2)}) copy-start(bf16[2,512,256]{1,2,0:T(8,128)(2,1)} %fusion.21) | copy-start | bytes 1572868
  88.9 25.9 %copy-start.4 = (f32[1024,256]{0,1:T(8,128)}, f32[1024,256]{0,1:T(8,128)S(1)}, u32[]{:S(2)}) copy-start(f32[1024,256]{0,1:T(8,128)S(1)} %get-tuple-element.54) | copy-start | bytes 3145732
  98.5 3.7 %collective-permute-start.9 = (f32[1,8,512]{2,1,0:T(8,128)S(1)}, f32[1,8,512]{2,1,0:T(8,128)S(1)}, u32[]{:S(2)}, u32[]{:S(2)}) collective-permute-start(f32[1,8,512]{2,1,0:T(8,128)S(1)} %bitcast.328), channel_id=1, source_target_pairs={{0,2},{1,3},{2,0},{3,1},{4,6},{5,7},{6,4},{7,5},{8,10},{9,11},{10,... | collective-permute-start | bytes 49160 | tf_op jit(solution)/shard_map/ppermute | solution.py:19
  98.5 34.4 %collective-permute-start.17 = (bf16[1,512,256]{1,2,0:T(8,128)(2,1)S(1)}, bf16[1,512,256]{1,2,0:T(8,128)(2,1)S(1)}, u32[]{:S(2)}, u32[]{:S(2)}) collective-permute-start(bf16[1,512,256]{1,2,0:T(8,128)(2,1)S(1)} %constant_dynamic-slice_fusion.2), channel_id=1, source_target_pairs={{0,1},{1,0},{2,3},{3,2},{4,5},{5,4},{6,7},{7,6},{8,9},{9,8},{10,11... | collective-permute-start | bytes 786440 | tf_op jit(solution)/shard_map/ppermute | solution.py:19
  99.1 15.6 %copy-start.3 = (f32[8,512,1024]{2,1,0:T(8,128)S(1)}, f32[8,512,1024]{2,1,0:T(8,128)}, u32[]{:S(2)}) copy-start(f32[8,512,1024]{2,1,0:T(8,128)} %get-tuple-element.56) | copy-start | bytes 50331652
  102.2 4.7 %collective-permute-start.10 = (f32[1,8,512]{2,1,0:T(8,128)S(1)}, f32[1,8,512]{2,1,0:T(8,128)S(1)}, u32[]{:S(2)}, u32[]{:S(2)}) collective-permute-start(f32[1,8,512]{2,1,0:T(8,128)S(1)} %bitcast_maximum_fusion), channel_id=1, source_target_pairs={{0,4},{1,5},{2,6},{3,7},{4,0},{5,1},{6,2},{7,3},{8,12},{9,13},{10,... | collective-permute-start | bytes 49160 | tf_op jit(solution)/shard_map/ppermute | solution.py:19
  106.9 26.1 %copy-start.7 = (bf16[2,512,256]{1,2,0:T(8,128)(2,1)S(1)}, bf16[2,512,256]{1,2,0:T(8,128)(2,1)}, u32[]{:S(2)}) copy-start(bf16[2,512,256]{1,2,0:T(8,128)(2,1)} %fusion.21) | copy-start | bytes 1572868
  118.4 4.6 %collective-permute-start.13 = (bf16[256,8]{0,1:T(8,128)(2,1)S(1)}, bf16[256,8]{0,1:T(8,128)(2,1)S(1)}, u32[]{:S(2)}, u32[]{:S(2)}) collective-permute-start(bf16[256,8]{0,1:T(8,128)(2,1)S(1)} %fusion.134), channel_id=1, source_target_pairs={{0,4},{1,5},{2,6},{3,7},{4,0},{5,1},{6,2},{7,3},{8,12},{9,13},{10,... | collective-permute-start | bytes 12296 | tf_op jit(solution)/shard_map/ppermute | solution.py:19
  118.7 5.8 %collective-permute-start.11 = (bf16[256,128]{1,0:T(8,128)(2,1)S(1)}, bf16[256,128]{1,0:T(8,128)(2,1)S(1)}, u32[]{:S(2)}, u32[]{:S(2)}) collective-permute-start(bf16[256,128]{1,0:T(8,128)(2,1)S(1)} %bitcast.331), channel_id=1, source_target_pairs={{0,4},{1,5},{2,6},{3,7},{4,0},{5,1},{6,2},{7,3},{8,12},{9,13},{10,... | collective-permute-start | bytes 196616 | tf_op jit(solution)/shard_map/ppermute | solution.py:19
  123.0 3.6 %collective-permute-start.14 = (bf16[128,8]{0,1:T(8,128)(2,1)S(1)}, bf16[128,8]{0,1:T(8,128)(2,1)S(1)}, u32[]{:S(2)}, u32[]{:S(2)}) collective-permute-start(bf16[128,8]{0,1:T(8,128)(2,1)S(1)} %fusion.140), channel_id=1, source_target_pairs={{0,2},{1,3},{2,0},{3,1},{4,6},{5,7},{6,4},{7,5},{8,10},{9,11},{10,... | collective-permute-start | bytes 6152 | tf_op jit(solution)/shard_map/ppermute | solution.py:19
  124.5 4.0 %collective-permute-start.12 = (bf16[128,128]{1,0:T(8,128)(2,1)S(1)}, bf16[128,128]{1,0:T(8,128)(2,1)S(1)}, u32[]{:S(2)}, u32[]{:S(2)}) collective-permute-start(bf16[128,128]{1,0:T(8,128)(2,1)S(1)} %fusion.108), channel_id=1, source_target_pairs={{0,2},{1,3},{2,0},{3,1},{4,6},{5,7},{6,4},{7,5},{8,10},{9,11},{10,... | collective-permute-start | bytes 98312 | tf_op jit(solution)/shard_map/ppermute | solution.py:19
  132.4 4.3 %collective-permute-start.15 = (bf16[128,256]{1,0:T(8,128)(2,1)S(1)}, bf16[128,256]{1,0:T(8,128)(2,1)S(1)}, u32[]{:S(2)}, u32[]{:S(2)}) collective-permute-start(bf16[128,256]{1,0:T(8,128)(2,1)S(1)} %divide_convert_fusion), channel_id=1, source_target_pairs={{0,2},{1,3},{2,0},{3,1},{4,6},{5,7},{6,4},{7,5},{8,10},{9,11},{10,... | collective-permute-start | bytes 196616 | tf_op jit(solution)/shard_map/ppermute | solution.py:19
  136.8 7.3 %collective-permute-start.16 = (bf16[256,256]{1,0:T(8,128)(2,1)S(1)}, bf16[256,256]{1,0:T(8,128)(2,1)S(1)}, u32[]{:S(2)}, u32[]{:S(2)}) collective-permute-start(bf16[256,256]{1,0:T(8,128)(2,1)S(1)} %pad_maximum_fusion.5), channel_id=1, source_target_pairs={{0,4},{1,5},{2,6},{3,7},{4,0},{5,1},{6,2},{7,3},{8,12},{9,13},{10,... | collective-permute-start | bytes 393224 | tf_op jit(solution)/shard_map/ppermute | solution.py:19
  149.5 5.5 %copy-start.5 = (f32[1024,256]{0,1:T(8,128)S(1)}, f32[1024,256]{0,1:T(8,128)}, u32[]{:S(2)}) copy-start(f32[1024,256]{0,1:T(8,128)} %copy-done.4) | copy-start | bytes 3145732
  149.5 9.0 %copy-start.13 = (pred[64]{0:T(512)(128)(4,1)S(1)}, pred[64]{0:T(512)(128)(4,1)}, u32[]{:S(2)}) copy-start(pred[64]{0:T(512)(128)(4,1)} %copy-done.12) | copy-start | bytes 196
  149.5 9.0 %copy-start.14 = (bf16[256,256]{1,0:T(8,128)(2,1)S(1)}, bf16[256,256]{1,0:T(8,128)(2,1)}, u32[]{:S(2)}) copy-start(bf16[256,256]{1,0:T(8,128)(2,1)} %param.25) | copy-start | bytes 393220
  149.6 24.1 %copy-start.1 = (bf16[2,512,1280]{2,1,0:T(8,128)(2,1)S(1)}, bf16[2,512,1280]{2,1,0:T(8,128)(2,1)}, u32[]{:S(2)}) copy-start(bf16[2,512,1280]{2,1,0:T(8,128)(2,1)} %param.13) | copy-start | bytes 7864324
  153.8 7.7 %copy-start.11 = (s32[2]{0:T(128)S(1)}, s32[2]{0:T(128)}, u32[]{:S(2)}) copy-start(s32[2]{0:T(128)} %dynamic_slice.103) | copy-start | bytes 28
  160.5 5.2 %collective-permute-start.18 = (bf16[1,64,512]{2,1,0:T(8,128)(2,1)S(1)}, bf16[1,64,512]{2,1,0:T(8,128)(2,1)S(1)}, u32[]{:S(2)}, u32[]{:S(2)}) collective-permute-start(bf16[1,64,512]{2,1,0:T(8,128)(2,1)S(1)} %bitcast.330), channel_id=1, source_target_pairs={{0,1},{1,0},{2,3},{3,2},{4,5},{5,4},{6,7},{7,6},{8,9},{9,8},{10,11... | collective-permute-start | bytes 196616 | tf_op jit(solution)/shard_map/ppermute | solution.py:19
where the time goes:
time: 175 us; the launch traced here: 174 us
  matrix products  62 us (35%)
  other arithmetic  33.3 us (19%)
  waiting for transfers between devices  33.3 us (19%)
  starting transfers between devices  22.5 us (13%)
  local copies, waits for them, and re-layouts  10.9 us (6%)
  blocking collectives  7.2 us (4%)
  between operations  4.43 us (3%)
    ppermute x19, waiting for transfers between devices, partner(): lax.ppermute(x, axis, [(i, i ^ 1 << distance) for i in range(lax.axis_siz...  33.3 us
    dot_general x19, matrix products, bdot(): return jnp.dot(left, right, preferred_element_type=jnp.float32)  28.9 us
    ppermute x19, starting transfers between devices, partner(): lax.ppermute(x, axis, [(i, i ^ 1 << distance) for i in range(lax.axis_siz...  22.5 us
    dot_general x2, matrix products, shards(): jnp.einsum('iqhd,ikhd->ihqk', query_heads, key_heads, preferred_element_t...  16.2 us
    reduce_sum x2, other arithmetic, shards(): totals = jnp.sum(weights.astype(jnp.float32), axis=-1)  15.6 us
    reduce_sum x2, other arithmetic, shards(): jnp.sum(weights_two.astype(jnp.float32), axis=-1)  8.36 us
    all_gather x1, blocking collectives, shards(): gathered = lax.all_gather(result, 'section', axis=0, tiled=True)  7.2 us
    dot_general x2, matrix products, shards(): jnp.einsum('ihqk,ikhd->iqhd', weights, value_heads, preferred_element_typ...  6.69 us
  transfers between devices with their start and end apart: 19, of which 14 were waited for; matrix products, arithmetic and copies ran while one was open for 23% of the time, Pallas kernels for 0%

commit v1 on v0

v1 whole, which is shorter than its diff:
```python
import functools
import math

import jax
import jax.numpy as jnp
from jax import lax
from jax.experimental import pallas as pl
from jax.experimental.pallas import tpu as pltpu
from jax.sharding import PartitionSpec as P

HEADS = 8
GRID = 64
IMG_PIX = 1024
TOKS_P = 8
LAYERS = 2


NORM_EPS = 0.01
MESH = pl.DeviceIdType.MESH


def norm_rows(values):
    center = values - jnp.mean(values, axis=-1, keepdims=True)
    spread = jnp.mean(center * center, axis=-1, keepdims=True)
    return center * lax.rsqrt(spread + NORM_EPS)


def fourier(coord_x, coord_y, pe_basis):
    phase = (2.0 * coord_x - 1.0)[..., None] * pe_basis[0] + (2.0 * coord_y - 1.0)[
        ..., None
    ] * pe_basis[1]
    phase = 2.0 * math.pi * phase
    return jnp.concatenate([jnp.sin(phase), jnp.cos(phase)], axis=-1)


def grid_code(first_pos, count, pe_basis):
    rows = count // GRID
    x = (jnp.arange(GRID, dtype=jnp.int32).astype(jnp.float32) + 0.5) / GRID
    y = ((first_pos // GRID + jnp.arange(rows, dtype=jnp.int32)).astype(jnp.float32) + 0.5) / GRID
    across = 2.0 * math.pi * ((2.0 * x - 1.0)[:, None] * pe_basis[0])[None]
    down = 2.0 * math.pi * ((2.0 * y - 1.0)[:, None] * pe_basis[1])[:, None]
    sin_a, cos_a, sin_d, cos_d = jnp.sin(across), jnp.cos(across), jnp.sin(down), jnp.cos(down)
    sines = sin_a * cos_d + cos_a * sin_d
    cosines = cos_a * cos_d - sin_a * sin_d
    return jnp.concatenate([sines, cosines], axis=-1).reshape(count, -1)


def start_tokens(box_rows, token_table, pe_basis):
    coords = (box_rows.astype(jnp.float32) + 0.5) / IMG_PIX
    corner_one = fourier(coords[:, 0], coords[:, 1], pe_basis)
    corner_two = fourier(coords[:, 2], coords[:, 3], pe_basis)
    slots = jnp.arange(TOKS_P)[None, :, None]
    tokens = token_table[None] + jnp.where(slots == TOKS_P - 2, corner_one[:, None, :], 0.0)
    tokens = tokens + jnp.where(slots == TOKS_P - 1, corner_two[:, None, :], 0.0)
    return tokens.reshape(-1, token_table.shape[-1])


def bdot(left, right):
    return jnp.dot(left, right, preferred_element_type=jnp.float32)


def make_hq(early_part, w_early):
    hq_part = jax.nn.gelu(bdot(early_part, w_early), approximate=False).astype(jnp.bfloat16)
    return lax.optimization_barrier(hq_part)


def tile_rows(rows, most):
    return min(rows, most)


def head_attend(queries, keys_ref, values_ref, key_rows, head_lanes, bias):
    total = None
    peaks = []
    for head in range(HEADS):
        picked = jnp.where(head_lanes == head, queries, jnp.zeros_like(queries))
        scores = lax.dot_general(
            picked, keys_ref[...], (((1,), (1,)), ((), ())), preferred_element_type=jnp.float32
        )
        if bias is not None:
            scores = scores + bias
        peak = jnp.max(scores, axis=-1, keepdims=True)
        weights = jnp.exp(scores - peak).astype(jnp.bfloat16)
        part = bdot(weights, values_ref[head, :key_rows])
        total = part if total is None else total + part
        peaks.append(peak)
    return total, peaks


def decode_kernel(
    members,
    final_ref,
    hq_ref,
    code_ref,
    tok0_ref,
    bias_ref,
    live_ref,
    win_ref,
    wout_ref,
    up_ref,
    down_ref,
    whyper_ref,
    out_ref,
    fin,
    hqs,
    img,
    tok,
    tok3b,
    vaug,
    q1,
    k1,
    q2,
    k2,
    part_a,
    part_l,
    lse,
    recv_a,
    recv_l,
    a1_all,
    swap_send,
    swap_recv,
    a_send,
    a_recv,
    l_send,
    l_recv,
    g_send,
    g_recv,
):
    me = lax.axis_index("img")
    bit = lax.rem(me, 2)
    rank = me // 2
    other = me + 1 - 2 * bit
    pos_dev = final_ref.shape[1]
    width = final_ref.shape[2]
    rows_all = tok.shape[0]
    own = rows_all // members
    held_pos = img.shape[0]
    inner = q1.shape[1]
    head_size = inner // HEADS
    scale = head_size ** (-0.5)

    def peer_rank(step):
        return lax.rem(rank + step, members)

    barrier = pltpu.get_barrier_semaphore()
    pl.semaphore_signal(barrier, inc=1, device_id={"img": other}, device_id_type=MESH)
    for step in range(1, members):
        pl.semaphore_signal(
            barrier, inc=1, device_id={"img": peer_rank(step) * 2 + bit}, device_id_type=MESH
        )
    pl.semaphore_wait(barrier, members)

    def send(src, dst, send_sem, recv_sem, target):
        copy = pltpu.make_async_remote_copy(
            src_ref=src,
            dst_ref=dst,
            send_sem=send_sem,
            recv_sem=recv_sem,
            device_id={"img": target},
            device_id_type=MESH,
        )
        copy.start()
        return copy

    swap_final = send(
        final_ref.at[1 - bit], fin.at[bit], swap_send.at[0], swap_recv.at[0], other
    )
    swap_hq = send(hq_ref.at[1 - bit], hqs.at[bit], swap_send.at[1], swap_recv.at[1], other)
    fin[bit] = final_ref[bit]
    hqs[bit] = hq_ref[bit]

    lane_head = lax.broadcasted_iota(jnp.int32, (1, inner), 1) // head_size
    lane = lax.broadcasted_iota(jnp.int32, (1, inner), 1)
    key_rows_max = vaug.shape[1]
    for head in range(HEADS):
        ones = jnp.where(lane_head == head, 1.0, 0.0)
        vaug[head, :, inner:] = jnp.broadcast_to(ones, (key_rows_max, inner)).astype(jnp.bfloat16)

    tok_tile = tile_rows(rows_all, 256)
    mlp_tile = tile_rows(rows_all, 256)
    pos_tile = tile_rows(held_pos, 256)

    def set_values(start, count, values):
        for head in range(HEADS):
            vaug[head, pl.ds(start, count), :inner] = jnp.where(
                lane_head == head, values, 0.0
            ).astype(jnp.bfloat16)

    def scaled(values):
        return (values.astype(jnp.bfloat16).astype(jnp.float32) * scale).astype(jnp.bfloat16)

    @pl.loop(0, rows_all // mlp_tile)
    def _(step):
        rows = pl.ds(pl.multiple_of(step * mlp_tile, mlp_tile), mlp_tile)
        start = tok0_ref[rows, :]
        tok[rows, :] = start
        q1[rows, :] = scaled(bdot(start.astype(jnp.bfloat16), win_ref[0, 0]))

    swap_final.wait()
    for half in range(2):
        img[half * pos_dev : (half + 1) * pos_dev, :] = fin[half].astype(jnp.float32)

    copies = []
    for layer in range(LAYERS):

        @pl.loop(0, held_pos // pos_tile)
        def _(step):
            start = pl.multiple_of(step * pos_tile, pos_tile)
            rows = pl.ds(start, pos_tile)
            here = img[rows, :]
            key_b = (here + code_ref[rows, :]).astype(jnp.bfloat16)
            k1[rows, :] = bdot(key_b, win_ref[layer, 1]).astype(jnp.bfloat16)
            q2[rows, :] = scaled(bdot(key_b, win_ref[layer, 3]))
            values = bdot(here.astype(jnp.bfloat16), win_ref[layer, 2])
            set_values(start, pos_tile, values)

        @pl.loop(0, rows_all // tok_tile)
        def _(step):
            rows = pl.ds(pl.multiple_of(step * tok_tile, tok_tile), tok_tile)
            total, peaks = head_attend(q1[rows, :], k1, vaug, held_pos, lane_head, None)
            sums = total[:, inner:]
            part_a[layer, rows, :] = (total[:, :inner] / sums).astype(jnp.bfloat16)
            logs = jnp.log(sums)
            compact = jnp.zeros((tok_tile, inner), jnp.float32)
            for head in range(HEADS):
                column = peaks[head] + logs[:, head * head_size : head * head_size + 1]
                compact = jnp.where(lane == head, column, compact)
            lse[rows, :] = compact

        turned = jnp.transpose(lse[...])[:HEADS, :]
        for peer in range(members):
            part_l[layer, peer] = turned[:, peer * own : (peer + 1) * own]
        waits = []
        for step in range(1, members):
            peer = peer_rank(step)
            target = peer * 2 + bit
            waits.append(
                (
                    send(
                        part_a.at[layer, pl.ds(pl.multiple_of(peer * own, own), own)],
                        recv_a.at[layer, step],
                        a_send.at[layer, step],
                        a_recv.at[layer, step],
                        target,
                    ),
                    send(
                        part_l.at[layer, peer],
                        recv_l.at[layer, step],
                        l_send.at[layer, step],
                        l_recv.at[layer, step],
                        target,
                    ),
                )
            )
        own_rows = pl.ds(pl.multiple_of(rank * own, own), own)
        blocks = [part_a[layer, own_rows, :]]
        marks = [part_l[layer, rank]]
        for step in range(1, members):
            waits[step - 1][0].wait_recv()
            waits[step - 1][1].wait_recv()
            blocks.append(recv_a[layer, step])
            marks.append(recv_l[layer, step])
        highest = functools.reduce(jnp.maximum, marks)
        shares = [jnp.exp(mark - highest) for mark in marks]
        whole = functools.reduce(jnp.add, shares)
        spread = jnp.where(
            lax.broadcasted_iota(jnp.int32, (HEADS, inner), 1) // head_size
            == lax.broadcasted_iota(jnp.int32, (HEADS, inner), 0),
            1.0,
            0.0,
        )
        mixed = None
        for block, share in zip(blocks, shares):
            factor = lax.dot_general(
                share / whole,
                spread,
                (((0,), (0,)), ((), ())),
                preferred_element_type=jnp.float32,
                precision=lax.Precision.HIGHEST,
            )
            term = factor * block.astype(jnp.float32)
            mixed = term if mixed is None else mixed + term
        a1_all[layer, own_rows, :] = mixed.astype(jnp.bfloat16)
        shared = []
        for step in range(1, members):
            shared.append(
                send(
                    a1_all.at[layer, own_rows],
                    a1_all.at[layer, own_rows],
                    g_send.at[layer, step],
                    g_recv.at[layer, step],
                    peer_rank(step) * 2 + bit,
                )
            )
        for pair in waits:
            pair[0].wait_send()
            pair[1].wait_send()
        for copy in shared:
            copy.wait()

        @pl.loop(0, rows_all // mlp_tile)
        def _(step):
            start = pl.multiple_of(step * mlp_tile, mlp_tile)
            rows = pl.ds(start, mlp_tile)
            two = norm_rows(tok[rows, :] + bdot(a1_all[layer, rows, :], wout_ref[layer, 0]))
            hidden = jax.nn.relu(bdot(two.astype(jnp.bfloat16), up_ref[layer])).astype(jnp.bfloat16)
            three = norm_rows(two + bdot(hidden, down_ref[layer]))
            tok[rows, :] = three
            three_b = three.astype(jnp.bfloat16)
            k2[rows, :] = bdot(three_b, win_ref[layer, 4]).astype(jnp.bfloat16)
            set_values(start, mlp_tile, bdot(three_b, win_ref[layer, 5]))
            if layer < LAYERS - 1:
                q1[rows, :] = scaled(bdot(three_b, win_ref[layer + 1, 0]))
            else:
                tok3b[rows, :] = three_b

        @pl.loop(0, held_pos // pos_tile)
        def _(step):
            rows = pl.ds(pl.multiple_of(step * pos_tile, pos_tile), pos_tile)
            total, _ = head_attend(q2[rows, :], k2, vaug, rows_all, lane_head, bias_ref[...])
            second = (total[:, :inner] / total[:, inner:]).astype(jnp.bfloat16)
            img[rows, :] = norm_rows(img[rows, :] + bdot(second, wout_ref[layer, 1]))

    swap_hq.wait()
    prompts = out_ref.shape[0]
    pick = jnp.where(
        lax.broadcasted_iota(jnp.int32, (prompts, rows_all), 1)
        == lax.broadcasted_iota(jnp.int32, (prompts, rows_all), 0) * TOKS_P + (TOKS_P - 3),
        1.0,
        0.0,
    ).astype(jnp.bfloat16)
    slots = bdot(pick, tok3b[...]).astype(jnp.bfloat16)
    hyper = bdot(slots, whyper_ref[...]).astype(jnp.bfloat16)
    for half in range(2):
        span = slice(half * pos_dev, (half + 1) * pos_dev)
        feats = (img[span, :] + hqs[half].astype(jnp.float32)).astype(jnp.bfloat16)
        logits = lax.dot_general(
            hyper, feats, (((1,), (1,)), ((), ())), preferred_element_type=jnp.float32
        ) * width ** (-0.5)
        out_ref[:, half, :] = jnp.where(live_ref[...] > 0.0, logits, 0.0).astype(jnp.bfloat16)


def run_decode(members, final, hq, code, tok0, bias, live, win, wout, up, down, whyper):
    pos_dev, width = final.shape[1:]
    held_pos = 2 * pos_dev
    rows_all = tok0.shape[0]
    own = rows_all // members
    inner = win.shape[-1]
    prompts = live.shape[0]
    f32, bf16 = jnp.float32, jnp.bfloat16
    vmem = pltpu.VMEM
    dma = pltpu.SemaphoreType.DMA
    return pl.pallas_call(
        functools.partial(decode_kernel, members),
        out_shape=jax.ShapeDtypeStruct((prompts, 2, pos_dev), bf16),
        in_specs=[pl.BlockSpec(memory_space=vmem)] * 11,
        out_specs=pl.BlockSpec(memory_space=vmem),
        scratch_shapes=[
            vmem((2, pos_dev, width), bf16),
            vmem((2, pos_dev, width), bf16),
            vmem((held_pos, width), f32),
            vmem((rows_all, width), f32),
            vmem((rows_all, width), bf16),
            vmem((HEADS, max(held_pos, rows_all), 2 * inner), bf16),
            vmem((rows_all, inner), bf16),
            vmem((held_pos, inner), bf16),
            vmem((held_pos, inner), bf16),
            vmem((rows_all, inner), bf16),
            vmem((LAYERS, rows_all, inner), bf16),
            vmem((LAYERS, members, HEADS, own), f32),
            vmem((rows_all, inner), f32),
            vmem((LAYERS, members, own, inner), bf16),
            vmem((LAYERS, members, HEADS, own), f32),
            vmem((LAYERS, rows_all, inner), bf16),
            dma((2,)),
            dma((2,)),
        ]
        + [dma((LAYERS, members))] * 6,
        compiler_params=pltpu.CompilerParams(
            collective_id=0, has_side_effects=True, vmem_limit_bytes=60 * 2**20
        ),
    )(final, hq, code, tok0, bias, live, win, wout, up, down, whyper)


def shards(
    early_feats,
    final_embed,
    prompt_counts,
    box_pixels,
    pair_table,
    token_table,
    pe_basis,
    w_early,
    attend_in,
    attend_out,
    mlp_up,
    mlp_down,
    w_hyper,
):
    images = early_feats.shape[0]
    pos_dev = early_feats.shape[1]
    prompts = box_pixels.shape[1]
    devices = lax.axis_size("img")
    my_index = lax.axis_index("img")
    my_section = lax.axis_index("section")
    members = devices // images
    my_bit = my_index % images
    first_pos = (my_index // images) * images * pos_dev
    mine = my_section * images + my_bit
    count = lax.dynamic_index_in_dim(prompt_counts, mine, 0, keepdims=False)
    boxes = lax.dynamic_index_in_dim(box_pixels, mine, 0, keepdims=False)
    hq = make_hq(early_feats, w_early)
    tok0 = start_tokens(boxes, token_table, pe_basis)
    code = grid_code(first_pos, images * pos_dev, pe_basis)
    slots = jnp.arange(prompts * TOKS_P, dtype=jnp.int32)[None, :] // TOKS_P
    bias = jnp.where(slots < count, 0.0, -jnp.inf).astype(jnp.float32)
    live = (jnp.arange(prompts, dtype=jnp.int32)[:, None] < count).astype(jnp.float32)
    masks = run_decode(
        members,
        final_embed,
        hq,
        code,
        tok0,
        bias,
        live,
        attend_in,
        attend_out,
        mlp_up,
        mlp_down,
        w_hyper,
    )
    keep = lax.dynamic_index_in_dim(masks, my_bit, 1, keepdims=False)
    sent = lax.dynamic_index_in_dim(masks, 1 - my_bit, 1, keepdims=False)
    got = lax.ppermute(sent, "img", [(i, i ^ 1) for i in range(devices)])
    result = jnp.stack([jnp.where(my_bit == 0, keep, got), jnp.where(my_bit == 0, got, keep)])
    gathered = lax.all_gather(result, "section", axis=0, tiled=True)
    outputs = lax.dynamic_slice_in_dim(pair_table, my_section * images, images, 0)
    return jnp.concatenate(
        [
            lax.dynamic_slice_in_dim(gathered, outputs[i], 1, 0).astype(jnp.float32)
            for i in range(images)
        ]
    )


def solution(mesh):
    placed = (
        P("section", "img", None),
        P("section", "img", None),
        P(),
        P(),
        P(),
        P(),
        P(),
        P(),
        P(),
        P(),
        P(),
        P(),
        P(),
    )
    return jax.shard_map(
        shards, mesh=mesh, in_specs=placed, out_specs=P("section", None, "img"), check_vma=False
    )
```

time: 175 us -> 104 us (0.59)
  Pallas kernels: 0 us -> 76.6 us
  matrix products: 62 us -> 4.76 us
  waiting for transfers between devices: 33.3 us -> 0.01 us
  other arithmetic: 33.3 us -> 6.55 us
  starting transfers between devices: 22.5 us -> 0.59 us
  local copies, waits for them, and re-layouts: 10.9 us -> 4.32 us
    pallas_call x0 -> x1, Pallas kernels: none -> 76.6 us  [run_decode(): pl.pallas_call(functools.partial(decode_kernel, members), out_shape=jax.S...]
    ppermute x19 -> x1, waiting for transfers between devices: 33.3 us -> 0.01 us  [shards(): got = lax.ppermute(sent, 'img', [(i, i ^ 1) for i in range(devices)])]
    dot_general x9 -> x0, matrix products: 33.1 us -> none  [the longest x2 16.2 us: shards(): jnp.einsum('iqhd,ikhd->ihqk', query_heads, key_heads, preferred_element_t...]
    reduce_sum x10 -> x0, other arithmetic: 26.1 us -> none  [the longest x2 15.6 us: shards(): totals = jnp.sum(weights.astype(jnp.float32), axis=-1)]
    dot_general x19 -> x1, matrix products: 28.9 us -> 4.76 us  [bdot(): return jnp.dot(left, right, preferred_element_type=jnp.float32)]
    ppermute x19 -> x1, starting transfers between devices: 22.5 us -> 0.59 us  [shards(): got = lax.ppermute(sent, 'img', [(i, i ^ 1) for i in range(devices)])]
    sin x2 -> x1, other arithmetic: 2.31 us -> 0.44 us  [fourier(): return jnp.concatenate([jnp.sin(phase), jnp.cos(phase)], axis=-1)]
  transfers between devices with their start and end apart: 19 -> 1, of which waited for: 14 -> 0; matrix products, arithmetic and copies ran while one was open for 23% -> 1% of each run, Pallas kernels for 0% -> 0%
where the time goes in v1:
time: 104 us
  Pallas kernels  76.6 us (74%)
  blocking collectives  7.2 us (7%)
  other arithmetic  6.55 us (6%)
  matrix products  4.76 us (5%)
  local copies, waits for them, and re-layouts  4.32 us (4%)
  between operations  3.81 us (4%)
    pallas_call x1, Pallas kernels, run_decode(): pl.pallas_call(functools.partial(decode_kernel, members), out_shape=jax.S...  76.6 us
    all_gather x1, blocking collectives, shards(): gathered = lax.all_gather(result, 'section', axis=0, tiled=True)  7.2 us
    dot_general x1, matrix products, bdot(): return jnp.dot(left, right, preferred_element_type=jnp.float32)  4.76 us
  transfers between devices with their start and end apart: 1, of which 0 were waited for; matrix products, arithmetic and copies ran while one was open for 1% of the time, Pallas kernels for 0%

profile of v1, /device:TPU:0, one launch (start us, length us, event | category | flops | bytes accessed | tf_op | source)
XLA Modules:
  0.0 103.9 jit_solution(2132254648981762458)
XLA Ops:
  0.0 0.0 copy-start
  0.1 1.4 %dynamic_slice.25 = s32[1]{0:T(128)} dynamic-slice(s32[8]{0:T(128)} %param.15, s32[]{:T(128)S(6)} %select_n.78), dynamic_slice_sizes={1} | dynamic-slice | bytes 12 | tf_op jit(solution)/shard_map/jit(dynamic_index_in_dim)/dynamic_slice | solution.py:409
  1.5 1.2 %fusion.21.live_ref = f32[64,1]{1,0:T(8,128)} fusion(s32[]{:T(128)} %bitcast.13), kind=kLoop, calls=%fused_computation.46 | loop fusion | flops 128 | bytes 260 | tf_op jit(solution)/shard_map/convert_element_type | solution.py:416
  2.6 1.1 %compare_select_fusion.bias_ref = f32[1,512]{1,0:T(1,128)} fusion(s32[]{:T(128)} %bitcast.13), kind=kLoop, calls=%fused_computation.50 | loop fusion | flops 5120 | bytes 2052 | tf_op jit(solution)/shard_map/jit(_where)/select_n | solution.py:415
  3.8 0.7 multiply_bitcast_fusion
  4.5 0.8 slice_bitcast_fusion.1
  5.2 0.1 broadcast_in_dim.66
  5.4 0.1 broadcast_in_dim.72
  5.5 0.0 copy-done
  5.5 4.8 %fusion.2.hq_ref = bf16[2,512,256]{2,1,0:T(8,128)(2,1)} fusion(bf16[2,512,1280]{2,1,0:T(8,128)(2,1)S(1)} %copy-done, bf16[1280,256]{1,0:T(8,128)(2,1)} %param.20), kind=kOutput, calls=%fused_computation.3 | convolution fusion | flops 688128000 | bytes 3801088 | tf_op jit(solution)/shard_map/dot_general | solution.py:59
  10.3 0.0 copy-start.1
  10.3 0.1 fusion.23
  10.4 0.4 fusion.18
  10.8 0.1 multiply_add_fusion
  11.0 1.0 %pad_maximum_fusion.code_ref = f32[1024,256]{1,0:T(8,128)} fusion(f32[1024,128]{1,0:T(8,128)S(1)} %bitcast.50, f32[1024,128]{1,0:T(8,128)S(1)} %bitcast.49), kind=kLoop, calls=%fused_computation.4 | loop fusion | flops 262144 | bytes 2097152 | tf_op jit(solution)/shard_map/concatenate | solution.py:45
  12.0 0.0 copy-done.1
  12.0 1.0 fusion.11.tok0_ref
  13.1 0.0 copy-start.2
  13.1 76.6 %shard_map.127 = bf16[64,2,512]{2,1,0:T(2,128)(2,1)} custom-call(bf16[2,512,256]{2,1,0:T(8,128)(2,1)} %final_ref.1, bf16[2,512,256]{2,1,0:T(8,128)(2,1)} %fusion.2.hq_ref, f32[1024,256]{1,0:T(8,128)} %pad_maximum_fusion.code_ref, f32[512,256]{1,0:T(8,128)} %fusion.11.tok0_ref, f32[1,512]{1,0:T(1,128)} %compare_select_fusion.bias_ref, ...), custom_call_target="tpu_custom_call" | custom-call | tf_op jit(solution)/shard_map/pallas_call | solution.py:352
  89.7 1.3 %constant_dynamic-slice_fusion.3 = (bf16[64,1,512]{2,1,0:T(2,128)(2,1)S(1)}, bf16[64,1,512]{2,1,0:T(2,128)(2,1)S(1)}) fusion(bf16[64,2,512]{2,1,0:T(2,128)(2,1)} %shard_map.127, s32[]{:T(128)S(6)} %select_n.83, s32[]{:T(128)S(6)} %select_n.84), kind=kLoop, calls=%fused_computation.59 | loop fusion | bytes 262152 | tf_op jit(solution)/shard_map/jit(dynamic_index_in_dim)/dynamic_slice | solution.py:431
  91.0 0.6 collective-permute-start
  91.6 0.0 copy-done.2
  91.6 0.1 dynamic_slice.28
  91.6 0.6 fusion.24
  95.9 0.0 collective-permute-done
  95.9 7.2 %all_gather.3 = bf16[8,64,512]{2,1,0:T(8,128)(2,1)S(1)} all-gather(bf16[2,64,512]{2,1,0:T(8,128)(2,1)S(1)} %pad_maximum_fusion.1), channel_id=1, replica_groups=mesh['section'=4,'img'=8] {'section'}, dimensions={0}, use_global_device_ids=true | all-gather | bytes 655360 | tf_op jit(solution)/shard_map/all_gather | solution.py:435
  103.1 0.7 maximum_convert_fusion
  (12 shorter events, 0.1 us)
Async XLA Ops:
  0.0 5.5 %copy-start = (bf16[2,512,1280]{2,1,0:T(8,128)(2,1)S(1)}, bf16[2,512,1280]{2,1,0:T(8,128)(2,1)}, u32[]{:S(2)}) copy-start(bf16[2,512,1280]{2,1,0:T(8,128)(2,1)} %param.13) | copy-start | bytes 7864324
  10.3 1.8 %copy-start.1 = (f32[8,256]{1,0:T(8,128)S(1)}, f32[8,256]{1,0:T(8,128)}, u32[]{:S(2)}) copy-start(f32[8,256]{1,0:T(8,128)} %param.18) | copy-start | bytes 24580
  13.1 78.5 %copy-start.2 = (s32[8]{0:T(128)S(1)}, s32[8]{0:T(128)}, u32[]{:S(2)}) copy-start(s32[8]{0:T(128)} %param.17) | copy-start | bytes 100
  91.0 4.9 %collective-permute-start = (bf16[64,512]{1,0:T(8,128)(2,1)S(1)}, bf16[64,512]{1,0:T(8,128)(2,1)S(1)}, u32[]{:S(2)}, u32[]{:S(2)}) collective-permute-start(bf16[64,512]{1,0:T(8,128)(2,1)S(1)} %bitcast.51), channel_id=1, source_target_pairs={{0,1},{1,0},{2,3},{3,2},{4,5},{5,4},{6,7},{7,6},{8,9},{9,8},{10,11... | collective-permute-start | bytes 196616 | tf_op jit(solution)/shard_map/ppermute | solution.py:433
